TPU v7x, 32 devices: a whole 2x2x4 slice. The times are simulated.
32 devices in a mesh: dp: 2 (over x), tm: 4 (over z), mp: 4 (over y, core).
Axes of the slice: x: 2, y: 2, z: 4, core: 2. Of those that a mesh axis runs over, the one named last changes fastest.
Arguments:
- features: bfloat16 [32, 576, 1024], P(('dp', 'tm'), 'mp'), parts along dimension 0, may hold values from -6 to 6
- queries: bfloat16 [2048, 1024], P(('dp', 'tm')), parts along dimension 0, may hold values from -6 to 6
- anchor_frame: int32 [2048], P(('dp', 'tm')), parts along dimension 0, may hold values from 0 to 15, as said below
- anchor_patch: int32 [2048], P(('dp', 'tm')), parts along dimension 0, may hold values from 0 to 575
- time_offset: float32 [2048, 8, 4], P(('dp', 'tm')), parts along dimension 0, may hold values from -1.99 to 1.99
- space_offset: float32 [2, 2048, 8, 4], P(None, ('dp', 'tm')), parts along dimension 1, may hold values from -3 to 3
- value_weight: bfloat16 [1024, 1024], replicated, may hold values from -0.1875 to 0.1875
- point_weight: bfloat16 [1024, 32], replicated, may hold values from -0.1875 to 0.1875
- point_bias: float32 [32], replicated, may hold values from -6 to 260
- output_weight: bfloat16 [1024, 1024], P('mp'), may hold values from -0.1875 to 0.1875
- project_weight: bfloat16 [1024, 3584], P(None, 'mp'), may hold values from -2 to 2
- norm_gain: float32 [3584], P('mp'), may hold values from 0.1 to 1.9
- query_weight: bfloat16 [3584, 3072], P(None, 'mp'), may hold values from -0.09375 to 0.09375
- query_bias: float32 [3072], P('mp'), may hold values from -6 to 40
- cache_weight: bfloat16 [3584, 1024], P(None, 'mp'), may hold values from -0.09375 to 0.09375
- cache_bias: float32 [1024], P('mp'), may hold values from -6 to 40
Outputs:
- attention: bfloat16 [2048, 3072], P(('dp', 'tm'), 'mp'), parts along dimension 0
- key_value: bfloat16 [2048, 1024], P(('dp', 'tm'), 'mp'), parts along dimension 0
There are 2 independent parts, one for each index of `dp`. A program takes and returns all parts, laid end to end along the dimension named above; an argument that names none is the same for every part. Nothing has to cross between parts.
Inputs may be any that keep to these rules, and one draw needn't show every extreme that they name: `anchor_frame`: the anchor frame of query q lies among the 4 frames that begin at (q // 256) * 4.
All inputs are finite; a program needn't handle non-finite values.
Results may differ from a plain program's by a relative error of at most 0.04.
Values may be sent and summed in bfloat16 or wider, within the bound.
A program may use at most 64 MiB of HBM per device.

v0:
```python
import jax
import jax.numpy as jnp
from jax import lax
from jax.sharding import PartitionSpec as P

AH = 8
POINTS = 4
GRID = 24
KVH = 4
HD = 128
GROUP = 7
rope_base = 1000000.0
epsilon = 1e-06
masked = -1e30


def with_halo(block, sides, width):
    for axis, dim in sides:
        count = lax.axis_size(axis)
        forward = [(i, i + 1) for i in range(count - 1)]
        backward = [(target, source) for source, target in forward]
        low = lax.ppermute(
            lax.slice_in_dim(block, block.shape[dim] - width, None, axis=dim), axis, forward
        )
        high = lax.ppermute(lax.slice_in_dim(block, 0, width, axis=dim), axis, backward)
        block = jnp.concatenate([low, block, high], axis=dim)
    return block


def rotate(vectors, positions):
    half_width = vectors.shape[-1] // 2
    frequency = rope_base ** (-2.0 * jnp.arange(half_width, dtype=jnp.float32) / vectors.shape[-1])
    angles = positions.astype(jnp.float32)[:, None] * frequency[None, :]
    cosine = jnp.cos(angles)[:, None, :]
    sine_part = jnp.sin(angles)[:, None, :]
    first_half = vectors[..., :half_width]
    second_half = vectors[..., half_width:]
    return jnp.concatenate(
        [
            first_half * cosine - second_half * sine_part,
            second_half * cosine + first_half * sine_part,
        ],
        axis=-1,
    )


def trilinear_corners(frame_pos, row_pos, column_pos, weight, frame_total, side):
    floor_frame = jnp.floor(frame_pos)
    floor_row = jnp.floor(row_pos)
    floor_column = jnp.floor(column_pos)
    frame_part = frame_pos - floor_frame
    row_part = row_pos - floor_row
    column_part = column_pos - floor_column
    frame_start = floor_frame.astype(jnp.int32)
    row_start = floor_row.astype(jnp.int32)
    column_start = floor_column.astype(jnp.int32)
    listing = []
    for frame_step in (0, 1):
        for row_step in (0, 1):
            for column_step in (0, 1):
                frame_cell = frame_start + frame_step
                row_cell = row_start + row_step
                column_cell = column_start + column_step
                portion = weight * (frame_part if frame_step else 1.0 - frame_part)
                portion = portion * (row_part if row_step else 1.0 - row_part)
                portion = portion * (column_part if column_step else 1.0 - column_part)
                inside = (
                    (frame_cell >= 0)
                    & (frame_cell < frame_total)
                    & (row_cell >= 0)
                    & (row_cell < side)
                )
                inside = inside & (column_cell >= 0) & (column_cell < side)
                portion = jnp.where(inside, portion, 0.0)
                patch_id = jnp.clip(row_cell, 0, side - 1) * side + jnp.clip(
                    column_cell, 0, side - 1
                )
                listing.append((frame_cell, patch_id, portion))
    return listing


def make_attend(query_turned, positions, head_map, scaling):

    def attend(state_in, members, first_row):
        key_rows, value_rows = members
        length = key_rows.shape[0]
        block_len = 512
        block_count = length // block_len
        key_blocks = key_rows.reshape(block_count, block_len, -1, HD)[:, :, head_map, :]
        value_blocks = value_rows.reshape(block_count, block_len, -1, HD)[:, :, head_map, :]
        block_starts = jnp.arange(block_count, dtype=jnp.int32) * block_len

        def advance(running, inputs):
            peak_score, denominator, numerator = running
            key_block, value_block, block_start = inputs
            scores = (
                jnp.einsum(
                    "qhd,nhd->hqn", query_turned, key_block, preferred_element_type=jnp.float32
                )
                * scaling
            )
            key_pos = block_start + jnp.arange(block_len, dtype=jnp.int32)
            allowed = key_pos[None, None, :] <= positions[None, :, None]
            scores = jnp.where(allowed, scores, masked)
            new_peak = jnp.maximum(peak_score, jnp.max(scores, axis=-1))
            weights = jnp.where(allowed, jnp.exp(scores - new_peak[..., None]), 0.0)
            rescale = jnp.exp(peak_score - new_peak)
            denominator = denominator * rescale + jnp.sum(weights, axis=-1)
            numerator = numerator * rescale[..., None] + jnp.einsum(
                "hqn,nhd->hqd",
                weights.astype(jnp.bfloat16),
                value_block,
                preferred_element_type=jnp.float32,
            )
            return ((new_peak, denominator, numerator), None)

        result, unused = lax.scan(advance, state_in, (key_blocks, value_blocks, block_starts))
        return result

    return attend


def local(
    features,
    queries,
    anchor_frame,
    anchor_patch,
    time_offset,
    space_offset,
    value_weight,
    point_weight,
    point_bias,
    output_weight,
    project_weight,
    norm_gain,
    query_weight,
    query_bias,
    cache_weight,
    cache_bias,
):
    groups = lax.axis_size("mp")
    group_index = lax.axis_index("mp")
    frame_index = lax.axis_index("tm")
    frames_here, patches_here, feature_width = features.shape
    rows_here = queries.shape[0]
    frame_total = frames_here * lax.axis_size("tm")
    patch_total = GRID * GRID
    head_width = feature_width // AH
    heads_here = AH // groups
    first_frame = frame_index * frames_here - 2
    projected = jnp.dot(
        features.reshape(frames_here * patches_here, feature_width),
        value_weight,
        preferred_element_type=jnp.float32,
    )
    projected = projected.astype(jnp.bfloat16).reshape(frames_here, patches_here, feature_width)
    logits = jnp.dot(queries, point_weight, preferred_element_type=jnp.float32) + point_bias
    point_share = jax.nn.softmax(logits.reshape(rows_here, AH, POINTS), axis=-1)
    frame_pos = anchor_frame.astype(jnp.float32)[:, None, None] + time_offset
    row_pos = (anchor_patch // GRID).astype(jnp.float32)[:, None, None] + space_offset[0]
    column_pos = (anchor_patch % GRID).astype(jnp.float32)[:, None, None] + space_offset[1]

    def own_slice(array):
        return lax.dynamic_slice_in_dim(array, group_index * heads_here, heads_here, 1)

    by_head = lax.all_to_all(projected, "mp", split_axis=2, concat_axis=1, tiled=True)
    padded = with_halo(by_head, (("tm", 0),), 2)
    lookup = padded.reshape(-1, heads_here, head_width)
    head_lane = jnp.arange(heads_here, dtype=jnp.int32)[None, :, None]
    running = jnp.zeros((rows_here, heads_here, head_width), jnp.float32)
    for frame_cell, patch_id, portion in trilinear_corners(
        own_slice(frame_pos),
        own_slice(row_pos),
        own_slice(column_pos),
        own_slice(point_share),
        frame_total,
        GRID,
    ):
        local_frame = jnp.clip(frame_cell - first_frame, 0, frames_here + 3)
        picked = lookup[local_frame * patch_total + patch_id, head_lane]
        running = running + jnp.sum(portion[..., None] * picked.astype(jnp.float32), axis=2)
    sampled = running.reshape(rows_here, heads_here * head_width).astype(jnp.bfloat16)
    head_terms = jnp.dot(sampled, output_weight, preferred_element_type=jnp.float32)
    head_mix = lax.psum(head_terms, "mp")
    abstract = (queries.astype(jnp.float32) + head_mix).astype(jnp.bfloat16)
    visual = jnp.dot(abstract, project_weight, preferred_element_type=jnp.float32)
    squares = lax.psum(jnp.sum(visual * visual, axis=1), "mp")
    model_width = query_weight.shape[0]
    normed = (visual * lax.rsqrt(squares / model_width + epsilon)[:, None] * norm_gain).astype(
        jnp.bfloat16
    )
    shard_piece = lax.all_gather(normed, "mp", axis=1, tiled=True)
    query_sum = jnp.dot(shard_piece, query_weight, preferred_element_type=jnp.float32)
    cache_sum = jnp.dot(shard_piece, cache_weight, preferred_element_type=jnp.float32)
    positions = frame_index * rows_here + jnp.arange(rows_here, dtype=jnp.int32)
    query_heads = query_weight.shape[1] // HD
    query_turned = rotate(
        (query_sum + query_bias).reshape(rows_here, query_heads, HD), positions
    ).astype(jnp.bfloat16)
    cache_heads = cache_weight.shape[1] // HD
    cache_state = (cache_sum + cache_bias).reshape(rows_here, cache_heads, HD)
    is_key = group_index * cache_heads + jnp.arange(cache_heads, dtype=jnp.int32) < KVH
    cache_state = jnp.where(is_key[None, :, None], rotate(cache_state, positions), cache_state)
    key_value = cache_state.reshape(rows_here, cache_heads * HD).astype(jnp.bfloat16)
    cache_all = lax.all_gather(key_value, "mp", axis=1, tiled=True)
    key_rows = cache_all[:, : KVH * HD]
    value_rows = cache_all[:, KVH * HD :]
    own_heads = (group_index * query_heads + jnp.arange(query_heads, dtype=jnp.int32)) // GROUP
    scaling = HD ** (-0.5)
    initial = (
        jnp.full((query_heads, rows_here), masked, jnp.float32),
        jnp.zeros((query_heads, rows_here), jnp.float32),
        jnp.zeros((query_heads, rows_here, HD), jnp.float32),
    )
    span_heads = min(KVH, (query_heads - 1) // GROUP + 2)
    lowest = jnp.minimum(group_index * query_heads // GROUP, KVH - span_heads)
    key_rows = lax.dynamic_slice_in_dim(key_rows, lowest * HD, span_heads * HD, 1)
    value_rows = lax.dynamic_slice_in_dim(value_rows, lowest * HD, span_heads * HD, 1)
    attend = make_attend(query_turned, positions, own_heads - lowest, scaling)
    peak_score, denominator, numerator = attend(
        initial,
        (
            lax.all_gather(key_rows, "tm", axis=0, tiled=True),
            lax.all_gather(value_rows, "tm", axis=0, tiled=True),
        ),
        jnp.int32(0),
    )
    attention = (
        (numerator / denominator[..., None])
        .transpose(1, 0, 2)
        .reshape(rows_here, query_heads * HD)
        .astype(jnp.bfloat16)
    )
    return (attention, key_value)


def solution(mesh):
    return jax.shard_map(
        local,
        mesh=mesh,
        in_specs=(
            P(("dp", "tm"), "mp", None),
            P(("dp", "tm"), None),
            P(("dp", "tm")),
            P(("dp", "tm")),
            P(("dp", "tm"), None, None),
            P(None, ("dp", "tm"), None, None),
            P(),
            P(),
            P(),
            P("mp", None),
            P(None, "mp"),
            P("mp"),
            P(None, "mp"),
            P("mp"),
            P(None, "mp"),
            P("mp"),
        ),
        out_specs=(P(("dp", "tm"), "mp"), P(("dp", "tm"), "mp")),
        check_vma=False,
    )
```

profile of v0, /device:TPU:0, one launch (start us, length us, event | category | flops | bytes accessed | tf_op | source)
XLA Modules:
  0.0 499.3 jit_solution(2481878164457223012)
XLA Ops:
  7.2 1.6 copy-done
  8.8 2.7 convolution_convert_fusion
  11.4 2.5 copy.67
  14.0 4.6 all-to-all-start
  19.2 0.9 copy.66
  20.1 24.9 %all-to-all-done = bf16[4,144,1024]{1,0,2:T(4,128)(2,1)} async-done(((bf16[4,144,1024]{1,0,2:T(4,128)(2,1)}), bf16[4,144,1024]{1,0,2:T(4,128)(2,1)}, u32[]{:S(2)}, u32[]{:S(2)}) %all-to-all-start) | async-done | bytes 1179680 | tf_op jit(solution)/shard_map/all_to_all | solution.py:166
  45.0 4.7 fusion.73
  49.8 3.5 copy.68
  53.3 5.1 %collective-permute-start = (bf16[2,576,256]{2,1,0:T(8,128)(2,1)}, bf16[2,576,256]{2,1,0:T(8,128)(2,1)}, u32[]{:S(2)}, u32[]{:S(2)}) collective-permute-start(bf16[2,576,256]{2,1,0:T(8,128)(2,1)} %bitcast.167), channel_id=1, source_target_pairs={{0,4},{4,8},{8,12},{1,5},{5,9},{9,13},{2,6},{6,10},{10,14},{3,7},{... | collective-permute-start | bytes 1769480 | tf_op jit(solution)/shard_map/ppermute | solution.py:22
  58.4 1.9 copy.70
  60.3 1.3 collective-permute-start.1
  62.7 0.9 copy.72
  63.6 0.9 copy.76
  64.5 0.9 copy.74
  66.4 0.9 copy.80
  67.3 0.9 copy.78
  69.2 0.9 copy.82
  70.1 0.9 copy.84
  72.0 3.1 copy.69
  75.1 1.8 collective-permute-done.1
  76.9 2.9 pad_maximum_fusion
  79.9 5.7 %reshape.215 = bf16[4608,2,128]{2,1,0:T(2,128)(2,1)} reshape(bf16[8,576,256]{2,1,0:T(8,128)(2,1)} %pad_maximum_fusion) | data formatting | bytes 4718592 | tf_op jit(solution)/shard_map/reshape | solution.py:168
  85.6 32.5 %gather_fusion = bf16[2048,128]{1,0:T(8,128)(2,1)} fusion(bf16[4608,2,128]{2,1,0:T(2,128)(2,1)} %reshape.215, s32[2048]{0:T(1024)S(1)} %reshape.224), kind=kCustom, calls=%fused_computation | custom fusion | bytes 1064960 | tf_op jit(solution)/shard_map/gather | solution.py:180
  118.1 32.4 %gather_fusion.1 = bf16[2048,128]{1,0:T(8,128)(2,1)} fusion(bf16[4608,2,128]{2,1,0:T(2,128)(2,1)} %reshape.215, s32[2048]{0:T(1024)S(1)} %reshape.230), kind=kCustom, calls=%fused_computation.1 | custom fusion | bytes 1064960 | tf_op jit(solution)/shard_map/gather | solution.py:180
  150.5 32.5 %gather_fusion.2 = bf16[2048,128]{1,0:T(8,128)(2,1)} fusion(bf16[4608,2,128]{2,1,0:T(2,128)(2,1)} %reshape.215, s32[2048]{0:T(1024)S(1)} %reshape.236), kind=kCustom, calls=%fused_computation.2 | custom fusion | bytes 1064960 | tf_op jit(solution)/shard_map/gather | solution.py:180
  183.0 32.3 %gather_fusion.3 = bf16[2048,128]{1,0:T(8,128)(2,1)} fusion(bf16[4608,2,128]{2,1,0:T(2,128)(2,1)} %reshape.215, s32[2048]{0:T(1024)S(1)} %reshape.242), kind=kCustom, calls=%fused_computation.3 | custom fusion | bytes 1064960 | tf_op jit(solution)/shard_map/gather | solution.py:180
  215.3 32.4 %gather_fusion.4 = bf16[2048,128]{1,0:T(8,128)(2,1)} fusion(bf16[4608,2,128]{2,1,0:T(2,128)(2,1)} %reshape.215, s32[2048]{0:T(1024)S(1)} %reshape.248), kind=kCustom, calls=%fused_computation.4 | custom fusion | bytes 1064960 | tf_op jit(solution)/shard_map/gather | solution.py:180
  247.7 32.3 %gather_fusion.5 = bf16[2048,128]{1,0:T(8,128)(2,1)} fusion(bf16[4608,2,128]{2,1,0:T(2,128)(2,1)} %reshape.215, s32[2048]{0:T(1024)S(1)} %reshape.254), kind=kCustom, calls=%fused_computation.5 | custom fusion | bytes 1064960 | tf_op jit(solution)/shard_map/gather | solution.py:180
  280.0 23.0 %gather_fusion.6 = bf16[2048,128]{1,0:T(8,128)(2,1)S(1)} fusion(bf16[4608,2,128]{2,1,0:T(2,128)(2,1)} %reshape.215, s32[2048]{0:T(1024)S(1)} %reshape.260), kind=kCustom, calls=%fused_computation.6 | custom fusion | bytes 1064960 | tf_op jit(solution)/shard_map/gather | solution.py:180
  303.0 22.9 %gather_fusion.7 = bf16[2048,128]{1,0:T(8,128)(2,1)S(1)} fusion(bf16[4608,2,128]{2,1,0:T(2,128)(2,1)} %reshape.215, s32[2048]{0:T(1024)S(1)} %reshape.266), kind=kCustom, calls=%fused_computation.7 | custom fusion | bytes 1064960 | tf_op jit(solution)/shard_map/gather | solution.py:180
  326.0 3.7 fusion.28
  329.7 3.3 fusion.26
  333.0 2.0 fusion.24
  335.0 2.0 fusion.22
  337.4 1.3 fusion.32
  339.1 36.6 %all-reduce.2.cloned.1.call-done = f32[256,1024]{1,0:T(8,128)} async-done(((f32[256,1024]{1,0:T(8,128)}), f32[256,1024]{1,0:T(8,128)}) %all-reduce.2.cloned.1.call-update) | async-done | bytes 1048592 | tf_op jit(solution)/shard_map/psum | solution.py:184
  375.7 2.6 multiply_reduce_fusion
  378.3 5.9 %psum.15 = f32[256]{0:T(256)S(1)} all-reduce(f32[256]{0:T(256)S(1)} %get-tuple-element.180), channel_id=1, replica_groups=mesh['dp'=2,'tm'=4,'mp'=4] {'mp'}, use_global_device_ids=true, to_apply=%region_12.13 | all-reduce | flops 256 | bytes 2048 | tf_op jit(solution)/shard_map/psum | solution.py:187
  384.3 0.9 multiply_convert_fusion
  386.9 19.8 %all-gather.2.cloned.1.call-done = bf16[256,3584]{1,0:T(8,128)(2,1)} async-done(((bf16[256,896]{1,0:T(8,128)(2,1)}), bf16[256,3584]{1,0:T(8,128)(2,1)}) %all-gather.2.cloned.1.call-update) | async-done | bytes 1835024 | tf_op jit(solution)/shard_map/all_gather | solution.py:192
  406.7 2.9 convolution_add_fusion.1
  409.8 7.2 %all_gather.13 = bf16[256,1024]{0,1:T(8,128)(2,1)S(1)} all-gather(bf16[256,256]{0,1:T(8,128)(2,1)S(1)} %fusion.31), channel_id=1, replica_groups=mesh['dp'=2,'tm'=4,'mp'=4] {'mp'}, dimensions={1}, use_global_device_ids=true | all-gather | bytes 655360 | tf_op jit(solution)/shard_map/all_gather | solution.py:205
  417.7 5.6 %convolution_add_fusion = f32[256,768]{1,0:T(8,128)} fusion(bf16[256,3584]{1,0:T(8,128)(2,1)} %all-gather.2.cloned.1.call-done, bf16[3584,768]{1,0:T(8,128)(2,1)} %param.30, f32[768]{0:T(1024)S(1)} %copy-done.23), kind=kOutput, calls=%fused_computation.39 | convolution fusion | flops 1409482752 | bytes 8129536 | tf_op jit(solution)/shard_map/dot_general | solution.py:193
  423.3 1.4 copy.87
  425.9 16.1 %all_gather.15 = bf16[1024,256]{0,1:T(8,128)(2,1)S(1)} all-gather(bf16[256,256]{0,1:T(8,128)(2,1)S(1)} %constant_dynamic-slice_fusion), channel_id=1, replica_groups=mesh['dp'=2,'tm'=4,'mp'=4] {'tm'}, dimensions={0}, use_global_device_ids=true | all-gather | bytes 655360 | tf_op jit(solution)/shard_map/all_gather | solution.py:224
  442.8 0.9 constant_dynamic-slice_fusion.1
  443.7 16.0 %all_gather.14 = bf16[1024,256]{0,1:T(8,128)(2,1)S(1)} all-gather(bf16[256,256]{0,1:T(8,128)(2,1)S(1)} %constant_dynamic-slice_fusion.1), channel_id=1, replica_groups=mesh['dp'=2,'tm'=4,'mp'=4] {'tm'}, dimensions={0}, use_global_device_ids=true | all-gather | bytes 655360 | tf_op jit(solution)/shard_map/all_gather | solution.py:223
  459.7 1.2 reshape.217
  460.9 1.4 copy.86
  462.2 2.1 gather_fusion.9
  464.3 2.1 gather_fusion.8
  466.4 23.6 %while.15 = (s32[]{:T(128)}, f32[6,256]{1,0:T(8,128)S(1)}, f32[6,256]{1,0:T(8,128)S(1)}, f32[6,256,128]{2,1,0:T(8,128)}, s32[2]{0:T(128)}, /*index=5*/bf16[2,512...) while((s32[]{:T(128)}, f32[6,256]{1,0:T(8,128)S(1)}, ...), condition=%wide.region_16.17_spmd.clone, body=%wide.region_13.16_spmd.clone.sunk | while | flops 413606144 | bytes 32480480 | solution.py:117
  466.4 1.2 dynamic_slice.139
  468.4 3.5 fusion.96
  471.9 2.8 fusion.97
  474.7 2.6 fusion.99
  477.3 0.9 copy-done.14
  478.2 1.2 dynamic_slice.139
  480.2 3.5 fusion.96
  483.7 2.8 fusion.97
  486.6 2.6 fusion.99
  489.1 0.9 copy-done.14
  490.0 1.4 copy.92
  491.5 0.9 copy.93
  (122 shorter events, 11.7 us)
Async XLA Ops:
  7.2 1.6 copy-start
  13.9 4.7 copy-start.2
  14.0 4.7 copy-start.17
  14.0 4.7 copy-start.22
  14.0 5.1 %copy-start.21 = (s32[256]{0:T(256)S(1)}, s32[256]{0:T(256)}, u32[]{:S(2)}) copy-start(s32[256]{0:T(256)} %param.20) | copy-start | bytes 3076
  14.0 5.1 %copy-start.20 = (s32[256]{0:T(256)S(1)}, s32[256]{0:T(256)}, u32[]{:S(2)}) copy-start(s32[256]{0:T(256)} %param.21) | copy-start | bytes 3076
  14.0 5.1 %copy-start.16 = (f32[2,256,8,4]{1,3,2,0:T(4,128)S(1)}, f32[2,256,8,4]{1,3,2,0:T(4,128)}, u32[]{:S(2)}) copy-start(f32[2,256,8,4]{1,3,2,0:T(4,128)} %param.23) | copy-start | bytes 196612
  14.0 5.1 %copy-start.18 = (f32[256,8,4]{0,2,1:T(4,128)S(1)}, f32[256,8,4]{0,2,1:T(4,128)}, u32[]{:S(2)}) copy-start(f32[256,8,4]{0,2,1:T(4,128)} %param.22) | copy-start | bytes 98308
  14.0 31.0 %all-to-all-start = ((bf16[4,144,1024]{1,0,2:T(4,128)(2,1)}), bf16[4,144,1024]{1,0,2:T(4,128)(2,1)}, u32[]{:S(2)}, u32[]{:S(2)}) async-start(bf16[4,144,1024]{1,0,2:T(4,128)(2,1)} %copy.67), calls=%async_computation | async-start | bytes 4194304 | tf_op jit(solution)/shard_map/all_to_all | solution.py:166
  18.6 357.1 %all-reduce.2.cloned.1.call-start = ((), (), s32[]{:S(2)}) async-start(), calls=%async_computation.1 | async-start | bytes 2097152 | tf_op jit(solution)/shard_map/psum | solution.py:184
  53.3 21.8 %collective-permute-start = (bf16[2,576,256]{2,1,0:T(8,128)(2,1)}, bf16[2,576,256]{2,1,0:T(8,128)(2,1)}, u32[]{:S(2)}, u32[]{:S(2)}) collective-permute-start(bf16[2,576,256]{2,1,0:T(8,128)(2,1)} %bitcast.167), channel_id=1, source_target_pairs={{0,4},{4,8},{8,12},{1,5},{5,9},{9,13},{2,6},{6,10},{10,14},{3,7},{... | collective-permute-start | bytes 1769480 | tf_op jit(solution)/shard_map/ppermute | solution.py:22
  60.3 16.7 %collective-permute-start.1 = (bf16[2,576,256]{2,1,0:T(8,128)(2,1)}, bf16[2,576,256]{2,1,0:T(8,128)(2,1)}, u32[]{:S(2)}, u32[]{:S(2)}) collective-permute-start(bf16[2,576,256]{2,1,0:T(8,128)(2,1)} %bitcast.168), channel_id=1, source_target_pairs={{4,0},{8,4},{12,8},{5,1},{9,5},{13,9},{6,2},{10,6},{14,10},{7,3},{... | collective-permute-start | bytes 1769480 | tf_op jit(solution)/shard_map/ppermute | solution.py:25
  303.0 22.9 %copy-start.8 = (f32[256,2,4]{2,1,0:T(2,128)S(1)}, f32[256,2,4]{2,1,0:T(2,128)}, u32[]{:S(2)}) copy-start(f32[256,2,4]{2,1,0:T(2,128)} %copy.66) | copy-start | bytes 24580
  325.9 3.8 copy-start.6
  325.9 3.8 copy-start.7
  325.9 7.0 %copy-start.4 = (bf16[2048,128]{1,0:T(8,128)(2,1)S(1)}, bf16[2048,128]{1,0:T(8,128)(2,1)}, u32[]{:S(2)}) copy-start(bf16[2048,128]{1,0:T(8,128)(2,1)} %gather_fusion.4) | copy-start | bytes 1572868
  325.9 7.0 %copy-start.5 = (bf16[2048,128]{1,0:T(8,128)(2,1)S(1)}, bf16[2048,128]{1,0:T(8,128)(2,1)}, u32[]{:S(2)}) copy-start(bf16[2048,128]{1,0:T(8,128)(2,1)} %gather_fusion.5) | copy-start | bytes 1572868
  325.9 7.0 %copy-start.9 = (f32[256,2,4]{2,1,0:T(2,128)S(1)}, f32[256,2,4]{2,1,0:T(2,128)}, u32[]{:S(2)}) copy-start(f32[256,2,4]{2,1,0:T(2,128)} %copy.80) | copy-start | bytes 24580
  325.9 7.0 %copy-start.10 = (f32[256,2,4]{2,1,0:T(2,128)S(1)}, f32[256,2,4]{2,1,0:T(2,128)}, u32[]{:S(2)}) copy-start(f32[256,2,4]{2,1,0:T(2,128)} %copy.78) | copy-start | bytes 24580
  329.6 5.4 %copy-start.11 = (f32[256,2,4]{2,1,0:T(2,128)S(1)}, f32[256,2,4]{2,1,0:T(2,128)}, u32[]{:S(2)}) copy-start(f32[256,2,4]{2,1,0:T(2,128)} %copy.82) | copy-start | bytes 24580
  329.6 5.4 %copy-start.12 = (f32[256,2,4]{2,1,0:T(2,128)S(1)}, f32[256,2,4]{2,1,0:T(2,128)}, u32[]{:S(2)}) copy-start(f32[256,2,4]{2,1,0:T(2,128)} %copy.84) | copy-start | bytes 24580
  335.0 2.5 copy-start.15
  337.0 38.7 %copy-start.3 = (bf16[256,1024]{1,0:T(8,128)(2,1)S(1)}, bf16[256,1024]{1,0:T(8,128)(2,1)}, u32[]{:S(2)}) copy-start(bf16[256,1024]{1,0:T(8,128)(2,1)} %param.19) | copy-start | bytes 1572868
  338.8 45.5 %copy-start.19 = (f32[896]{0:T(1024)S(1)}, f32[896]{0:T(1024)}, u32[]{:S(2)}) copy-start(f32[896]{0:T(1024)} %param.29) | copy-start | bytes 10756
  338.8 67.9 %all-gather.2.cloned.1.call-start = ((), (), s32[]{:S(2)}) async-start(), calls=%async_computation.2 | async-start | bytes 2293760 | tf_op jit(solution)/shard_map/all_gather | solution.py:192
  386.9 30.8 %copy-start.23 = (f32[768]{0:T(1024)S(1)}, f32[768]{0:T(1024)}, u32[]{:S(2)}) copy-start(f32[768]{0:T(1024)} %param.31) | copy-start | bytes 9220
  468.4 6.3 %copy-start.13 = (f32[6,256,128]{2,1,0:T(8,128)S(1)}, f32[6,256,128]{2,1,0:T(8,128)}, u32[]{:S(2)}) copy-start(f32[6,256,128]{2,1,0:T(8,128)} %get-tuple-element.267) | copy-start | bytes 2359300 | tf_op jit(solution)/shard_map/while
  471.9 2.8 copy-start.1
  477.3 0.9 copy-start.14
  480.2 6.3 %copy-start.13 = (f32[6,256,128]{2,1,0:T(8,128)S(1)}, f32[6,256,128]{2,1,0:T(8,128)}, u32[]{:S(2)}) copy-start(f32[6,256,128]{2,1,0:T(8,128)} %get-tuple-element.267) | copy-start | bytes 2359300 | tf_op jit(solution)/shard_map/while
  483.7 2.8 copy-start.1
  489.1 0.9 copy-start.14
Sparse Core Ops, SparseCore 0:
  338.9 36.7 all-reduce.1
  385.4 21.2 all-gather.1
where the time goes:
time: 502 us; the launch traced here: 499 us
  local copies, waits for them, and re-layouts  293 us (58%)
  waiting for transfers between devices  83.2 us (17%)
  blocking collectives  45.1 us (9%)
  matrix products  27.4 us (5%)
  other arithmetic  24.5 us (5%)
  between operations  14.8 us (3%)
  starting transfers between devices  11.3 us (2%)
    gather x8, local copies, waits for them, and re-layouts, local(): picked = lookup[local_frame * patch_total + patch_id, head_lane]  240 us
    psum x1, waiting for transfers between devices, local(): head_mix = lax.psum(head_terms, 'mp')  36.6 us
    all_to_all x1, waiting for transfers between devices, local(): lax.all_to_all(projected, 'mp', split_axis=2, concat_axis=1, tiled=True)  24.9 us
    all_gather x1, waiting for transfers between devices, local(): shard_piece = lax.all_gather(normed, 'mp', axis=1, tiled=True)  19.8 us
    all_gather x1, blocking collectives, local(): lax.all_gather(value_rows, 'tm', axis=0, tiled=True)  16.1 us
    all_gather x1, blocking collectives, local(): lax.all_gather(key_rows, 'tm', axis=0, tiled=True)  16 us
    reduce_sum x4, other arithmetic, local(): jnp.sum(portion[..., None] * picked.astype(jnp.float32), axis=2)  10.9 us
  transfers between devices with their start and end apart: 5, of which 4 were waited for; matrix products, arithmetic and copies ran while one was open for 4% of the time, Pallas kernels for 0%

commit v1 on v0

--- a/solution.py
+++ b/solution.py
@@ -163,7 +163,19 @@
     def own_slice(array):
         return lax.dynamic_slice_in_dim(array, group_index * heads_here, heads_here, 1)
 
-    by_head = lax.all_to_all(projected, "mp", split_axis=2, concat_axis=1, tiled=True)
+    ways, here = (lax.axis_size("mp"), lax.axis_index("mp"))
+    width_2 = projected.shape[2] // ways
+    lengths = list(projected.shape)
+    lengths[2] = width_2
+    height = lengths[1]
+    lengths[1] = height * ways
+    full = jnp.zeros(lengths, projected.dtype)
+    for mask in range(ways):
+        part = lax.dynamic_slice_in_dim(projected, (here ^ mask) * width_2, width_2, axis=2)
+        if mask:
+            part = lax.ppermute(part, "mp", [(d, d ^ mask) for d in range(ways)])
+        full = lax.dynamic_update_slice_in_dim(full, part, (here ^ mask) * height, axis=1)
+    by_head = full
     padded = with_halo(by_head, (("tm", 0),), 2)
     lookup = padded.reshape(-1, heads_here, head_width)
     head_lane = jnp.arange(heads_here, dtype=jnp.int32)[None, :, None]

time: 502 us -> 483 us (0.962)
  waiting for transfers between devices: 83.2 us -> 64.1 us
    all_to_all x1 -> x0, waiting for transfers between devices: 24.9 us -> none  [local(): lax.all_to_all(projected, 'mp', split_axis=2, concat_axis=1, tiled=True)]
    concatenate x16, local copies, waits for them, and re-layouts: 4.14 us -> 17.1 us  [local(): picked = lookup[local_frame * patch_total + patch_id, head_lane]]
    slice x2 -> x1, local copies, waits for them, and re-layouts: 8.29 us -> 1.1 us  [with_halo(): lax.slice_in_dim(block, block.shape[dim] - width, None, axis=dim)]
    ppermute x0 -> x3, waiting for transfers between devices: none -> 5.56 us  [local(): part = lax.ppermute(part, 'mp', [(d, d ^ mask) for d in range(ways)])]
  transfers between devices with their start and end apart: 5 -> 7, of which waited for: 4 -> 4; matrix products, arithmetic and copies ran while one was open for 4% -> 6% of each run, Pallas kernels for 0% -> 0%
where the time goes in v1:
time: 483 us; the launch traced here: 480 us
  local copies, waits for them, and re-layouts  294 us (61%)
  waiting for transfers between devices  64.1 us (13%)
  blocking collectives  45.1 us (9%)
  matrix products  28.5 us (6%)
  other arithmetic  24.5 us (5%)
  between operations  14.8 us (3%)
  starting transfers between devices  8.92 us (2%)
    gather x8, local copies, waits for them, and re-layouts, local(): picked = lookup[local_frame * patch_total + patch_id, head_lane]  240 us
    psum x1, waiting for transfers between devices, local(): head_mix = lax.psum(head_terms, 'mp')  38.6 us
    all_gather x1, waiting for transfers between devices, local(): shard_piece = lax.all_gather(normed, 'mp', axis=1, tiled=True)  19.9 us
    concatenate x16, local copies, waits for them, and re-layouts, local(): picked = lookup[local_frame * patch_total + patch_id, head_lane]  17.1 us
    all_gather x1, blocking collectives, local(): lax.all_gather(value_rows, 'tm', axis=0, tiled=True)  16.1 us
    all_gather x1, blocking collectives, local(): lax.all_gather(key_rows, 'tm', axis=0, tiled=True)  16 us
  transfers between devices with their start and end apart: 7, of which 4 were waited for; matrix products, arithmetic and copies ran while one was open for 6% of the time, Pallas kernels for 0%

profile of v1, /device:TPU:0, one launch (start us, length us, event | category | flops | bytes accessed | tf_op | source)
XLA Modules:
  0.0 480.2 jit_solution(1775927877947702237)
XLA Ops:
  7.2 1.5 copy-done
  8.8 2.7 convolution_convert_fusion
  11.6 1.0 constant_dynamic-slice_fusion.2
  13.0 2.5 collective-permute-start.1
  15.7 1.3 convolution_add_fusion.2
  18.7 1.3 reshape.222
  20.9 1.3 reshape.228
  22.1 1.0 constant_dynamic-update-slice_fusion.2
  23.7 1.0 constant_dynamic-update-slice_fusion.1
  24.7 5.0 %collective-permute-done.2 = bf16[4,144,256]{2,1,0:T(8,128)(2,1)} collective-permute-done((bf16[4,144,256]{2,1,0:T(8,128)(2,1)}, bf16[4,144,256]{2,1,0:T(8,128)(2,1)}, u32[]{:S(2)}, u32[]{:S(2)}) %collective-permute-start.2) | collective-permute-done | bytes 294944 | tf_op jit(solution)/shard_map/ppermute | solution.py:176
  29.7 1.0 constant_dynamic-update-slice_fusion
  30.7 1.1 fusion.73
  31.8 4.2 collective-permute-start.3
  36.0 1.3 collective-permute-start.4
  39.9 1.3 reshape.234
  42.0 1.3 reshape.240
  46.7 1.3 reshape.246
  48.8 1.3 reshape.252
  52.7 1.3 reshape.258
  53.9 0.9 copy.46
  56.5 1.3 reshape.264
  57.8 2.9 pad_maximum_fusion
  60.8 5.7 %reshape.213 = bf16[4608,2,128]{2,1,0:T(2,128)(2,1)} reshape(bf16[8,576,256]{2,1,0:T(8,128)(2,1)} %pad_maximum_fusion) | data formatting | bytes 4718592 | tf_op jit(solution)/shard_map/reshape | solution.py:180
  66.5 32.1 %gather_fusion = bf16[2048,128]{1,0:T(8,128)(2,1)} fusion(bf16[4608,2,128]{2,1,0:T(2,128)(2,1)} %reshape.213, s32[2048]{0:T(1024)S(1)} %reshape.222), kind=kCustom, calls=%fused_computation | custom fusion | bytes 1064960 | tf_op jit(solution)/shard_map/gather | solution.py:192
  98.6 32.3 %gather_fusion.1 = bf16[2048,128]{1,0:T(8,128)(2,1)} fusion(bf16[4608,2,128]{2,1,0:T(2,128)(2,1)} %reshape.213, s32[2048]{0:T(1024)S(1)} %reshape.228), kind=kCustom, calls=%fused_computation.1 | custom fusion | bytes 1064960 | tf_op jit(solution)/shard_map/gather | solution.py:192
  130.9 32.3 %gather_fusion.2 = bf16[2048,128]{1,0:T(8,128)(2,1)} fusion(bf16[4608,2,128]{2,1,0:T(2,128)(2,1)} %reshape.213, s32[2048]{0:T(1024)S(1)} %reshape.234), kind=kCustom, calls=%fused_computation.2 | custom fusion | bytes 1064960 | tf_op jit(solution)/shard_map/gather | solution.py:192
  163.3 32.4 %gather_fusion.3 = bf16[2048,128]{1,0:T(8,128)(2,1)} fusion(bf16[4608,2,128]{2,1,0:T(2,128)(2,1)} %reshape.213, s32[2048]{0:T(1024)S(1)} %reshape.240), kind=kCustom, calls=%fused_computation.3 | custom fusion | bytes 1064960 | tf_op jit(solution)/shard_map/gather | solution.py:192
  195.6 32.3 %gather_fusion.4 = bf16[2048,128]{1,0:T(8,128)(2,1)} fusion(bf16[4608,2,128]{2,1,0:T(2,128)(2,1)} %reshape.213, s32[2048]{0:T(1024)S(1)} %reshape.246), kind=kCustom, calls=%fused_computation.4 | custom fusion | bytes 1064960 | tf_op jit(solution)/shard_map/gather | solution.py:192
  227.9 32.3 %gather_fusion.5 = bf16[2048,128]{1,0:T(8,128)(2,1)} fusion(bf16[4608,2,128]{2,1,0:T(2,128)(2,1)} %reshape.213, s32[2048]{0:T(1024)S(1)} %reshape.252), kind=kCustom, calls=%fused_computation.5 | custom fusion | bytes 1064960 | tf_op jit(solution)/shard_map/gather | solution.py:192
  260.2 23.0 %gather_fusion.6 = bf16[2048,128]{1,0:T(8,128)(2,1)S(1)} fusion(bf16[4608,2,128]{2,1,0:T(2,128)(2,1)} %reshape.213, s32[2048]{0:T(1024)S(1)} %reshape.258), kind=kCustom, calls=%fused_computation.6 | custom fusion | bytes 1064960 | tf_op jit(solution)/shard_map/gather | solution.py:192
  283.2 23.0 %gather_fusion.7 = bf16[2048,128]{1,0:T(8,128)(2,1)S(1)} fusion(bf16[4608,2,128]{2,1,0:T(2,128)(2,1)} %reshape.213, s32[2048]{0:T(1024)S(1)} %reshape.264), kind=kCustom, calls=%fused_computation.7 | custom fusion | bytes 1064960 | tf_op jit(solution)/shard_map/gather | solution.py:192
  306.3 3.7 fusion.28
  310.0 2.0 fusion.26
  312.1 2.0 fusion.24
  314.1 2.0 fusion.22
  316.5 1.3 fusion.32
  318.1 38.6 %all-reduce.2.cloned.1.call-done = f32[256,1024]{1,0:T(8,128)} async-done(((f32[256,1024]{1,0:T(8,128)}), f32[256,1024]{1,0:T(8,128)}) %all-reduce.2.cloned.1.call-update) | async-done | bytes 1048592 | tf_op jit(solution)/shard_map/psum | solution.py:196
  356.7 2.6 multiply_reduce_fusion
  359.3 5.9 %psum.15 = f32[256]{0:T(256)S(1)} all-reduce(f32[256]{0:T(256)S(1)} %get-tuple-element.173), channel_id=1, replica_groups=mesh['dp'=2,'tm'=4,'mp'=4] {'mp'}, use_global_device_ids=true, to_apply=%region_12.13 | all-reduce | flops 256 | bytes 2048 | tf_op jit(solution)/shard_map/psum | solution.py:199
  365.3 0.9 multiply_convert_fusion
  367.8 19.9 %all-gather.2.cloned.1.call-done = bf16[256,3584]{1,0:T(8,128)(2,1)} async-done(((bf16[256,896]{1,0:T(8,128)(2,1)}), bf16[256,3584]{1,0:T(8,128)(2,1)}) %all-gather.2.cloned.1.call-update) | async-done | bytes 1835024 | tf_op jit(solution)/shard_map/all_gather | solution.py:204
  387.7 2.9 convolution_add_fusion.1
  390.8 7.2 %all_gather.13 = bf16[256,1024]{0,1:T(8,128)(2,1)S(1)} all-gather(bf16[256,256]{0,1:T(8,128)(2,1)S(1)} %fusion.31), channel_id=1, replica_groups=mesh['dp'=2,'tm'=4,'mp'=4] {'mp'}, dimensions={1}, use_global_device_ids=true | all-gather | bytes 655360 | tf_op jit(solution)/shard_map/all_gather | solution.py:217
  398.7 5.6 %convolution_add_fusion = f32[256,768]{1,0:T(8,128)} fusion(bf16[256,3584]{1,0:T(8,128)(2,1)} %all-gather.2.cloned.1.call-done, bf16[3584,768]{1,0:T(8,128)(2,1)} %param.30, f32[768]{0:T(1024)S(1)} %copy-done.24), kind=kOutput, calls=%fused_computation.39 | convolution fusion | flops 1409482752 | bytes 8129536 | tf_op jit(solution)/shard_map/dot_general | solution.py:205
  404.3 1.4 copy.51
  406.9 16.1 %all_gather.15 = bf16[1024,256]{0,1:T(8,128)(2,1)S(1)} all-gather(bf16[256,256]{0,1:T(8,128)(2,1)S(1)} %constant_dynamic-slice_fusion), channel_id=1, replica_groups=mesh['dp'=2,'tm'=4,'mp'=4] {'tm'}, dimensions={0}, use_global_device_ids=true | all-gather | bytes 655360 | tf_op jit(solution)/shard_map/all_gather | solution.py:236
  423.8 0.9 constant_dynamic-slice_fusion.1
  424.7 16.0 %all_gather.14 = bf16[1024,256]{0,1:T(8,128)(2,1)S(1)} all-gather(bf16[256,256]{0,1:T(8,128)(2,1)S(1)} %constant_dynamic-slice_fusion.1), channel_id=1, replica_groups=mesh['dp'=2,'tm'=4,'mp'=4] {'tm'}, dimensions={0}, use_global_device_ids=true | all-gather | bytes 655360 | tf_op jit(solution)/shard_map/all_gather | solution.py:235
  440.7 1.2 reshape.215
  441.9 1.4 copy.50
  443.3 2.1 gather_fusion.9
  445.4 2.1 gather_fusion.8
  447.4 23.5 %while.15 = (s32[]{:T(128)}, f32[6,256]{1,0:T(8,128)S(1)}, f32[6,256]{1,0:T(8,128)S(1)}, f32[6,256,128]{2,1,0:T(8,128)}, s32[2]{0:T(128)}, /*index=5*/bf16[2,512...) while((s32[]{:T(128)}, f32[6,256]{1,0:T(8,128)S(1)}, ...), condition=%wide.region_16.17_spmd.clone, body=%wide.region_13.16_spmd.clone.sunk | while | flops 413606144 | bytes 32480480 | solution.py:117
  447.4 1.2 dynamic_slice.159
  449.4 3.5 fusion.96
  452.9 2.8 fusion.97
  455.7 2.6 fusion.99
  459.2 1.2 dynamic_slice.159
  461.2 3.5 fusion.96
  464.7 2.8 fusion.97
  467.5 2.6 fusion.99
  470.1 0.9 copy-done.15
  471.0 1.4 copy.56
  472.5 0.9 copy.57
  (129 shorter events, 23.6 us)
Async XLA Ops:
  7.2 1.6 copy-start
  7.2 349.5 %all-reduce.2.cloned.1.call-start = ((), (), s32[]{:S(2)}) async-start(), calls=%async_computation | async-start | bytes 2097152 | tf_op jit(solution)/shard_map/psum | solution.py:196
  11.4 4.2 copy-start.18
  11.4 4.2 copy-start.23
  11.4 5.6 %copy-start.17 = (f32[2,256,8,4]{1,3,2,0:T(4,128)S(1)}, f32[2,256,8,4]{1,3,2,0:T(4,128)}, u32[]{:S(2)}) copy-start(f32[2,256,8,4]{1,3,2,0:T(4,128)} %param.23) | copy-start | bytes 196612
  11.5 5.6 %copy-start.21 = (s32[256]{0:T(256)S(1)}, s32[256]{0:T(256)}, u32[]{:S(2)}) copy-start(s32[256]{0:T(256)} %param.21) | copy-start | bytes 3076
  11.5 5.7 %copy-start.22 = (s32[256]{0:T(256)S(1)}, s32[256]{0:T(256)}, u32[]{:S(2)}) copy-start(s32[256]{0:T(256)} %param.20) | copy-start | bytes 3076
  11.5 5.7 %copy-start.19 = (f32[256,8,4]{0,2,1:T(4,128)S(1)}, f32[256,8,4]{0,2,1:T(4,128)}, u32[]{:S(2)}) copy-start(f32[256,8,4]{0,2,1:T(4,128)} %param.22) | copy-start | bytes 98308
  12.6 9.6 %collective-permute-start = (bf16[4,144,256]{2,1,0:T(8,128)(2,1)}, bf16[4,144,256]{2,1,0:T(8,128)(2,1)}, u32[]{:S(2)}, u32[]{:S(2)}) collective-permute-start(bf16[4,144,256]{2,1,0:T(8,128)(2,1)} %get-tuple-element.144), channel_id=1, source_target_pairs={{0,1},{1,0},{2,3},{3,2},{4,5},{5,4},{6,7},{7,6},{8,9},{9,8},{10,11... | collective-permute-start | bytes 884744 | tf_op jit(solution)/shard_map/ppermute | solution.py:176
  13.0 10.7 %collective-permute-start.1 = (bf16[4,144,256]{2,1,0:T(8,128)(2,1)}, bf16[4,144,256]{2,1,0:T(8,128)(2,1)}, u32[]{:S(2)}, u32[]{:S(2)}) collective-permute-start(bf16[4,144,256]{2,1,0:T(8,128)(2,1)} %get-tuple-element.143), channel_id=1, source_target_pairs={{0,2},{1,3},{2,0},{3,1},{4,6},{5,7},{6,4},{7,5},{8,10},{9,11},{10,... | collective-permute-start | bytes 884744 | tf_op jit(solution)/shard_map/ppermute | solution.py:176
  15.6 14.1 %collective-permute-start.2 = (bf16[4,144,256]{2,1,0:T(8,128)(2,1)}, bf16[4,144,256]{2,1,0:T(8,128)(2,1)}, u32[]{:S(2)}, u32[]{:S(2)}) collective-permute-start(bf16[4,144,256]{2,1,0:T(8,128)(2,1)} %get-tuple-element.142), channel_id=1, source_target_pairs={{0,3},{1,2},{2,1},{3,0},{4,7},{5,6},{6,5},{7,4},{8,11},{9,10},{10,... | collective-permute-start | bytes 884744 | tf_op jit(solution)/shard_map/ppermute | solution.py:176
  31.8 26.1 %collective-permute-start.3 = (bf16[2,576,256]{2,1,0:T(8,128)(2,1)}, bf16[2,576,256]{2,1,0:T(8,128)(2,1)}, u32[]{:S(2)}, u32[]{:S(2)}) collective-permute-start(bf16[2,576,256]{2,1,0:T(8,128)(2,1)} %get-tuple-element.140), channel_id=1, source_target_pairs={{0,4},{4,8},{8,12},{1,5},{5,9},{9,13},{2,6},{6,10},{10,14},{3,7},{... | collective-permute-start | bytes 1769480 | tf_op jit(solution)/shard_map/ppermute | solution.py:22
  36.0 21.8 %collective-permute-start.4 = (bf16[2,576,256]{2,1,0:T(8,128)(2,1)}, bf16[2,576,256]{2,1,0:T(8,128)(2,1)}, u32[]{:S(2)}, u32[]{:S(2)}) collective-permute-start(bf16[2,576,256]{2,1,0:T(8,128)(2,1)} %get-tuple-element.141), channel_id=1, source_target_pairs={{4,0},{8,4},{12,8},{5,1},{9,5},{13,9},{6,2},{10,6},{14,10},{7,3},{... | collective-permute-start | bytes 1769480 | tf_op jit(solution)/shard_map/ppermute | solution.py:25
  283.2 23.0 %copy-start.7 = (f32[256,2,4]{2,1,0:T(2,128)S(1)}, f32[256,2,4]{2,1,0:T(2,128)}, u32[]{:S(2)}) copy-start(f32[256,2,4]{2,1,0:T(2,128)} %copy.34) | copy-start | bytes 24580
  306.2 3.8 copy-start.5
  306.2 3.8 copy-start.6
  306.2 3.8 copy-start.8
  306.2 3.8 copy-start.9
  306.2 5.8 %copy-start.3 = (bf16[2048,128]{1,0:T(8,128)(2,1)S(1)}, bf16[2048,128]{1,0:T(8,128)(2,1)}, u32[]{:S(2)}) copy-start(bf16[2048,128]{1,0:T(8,128)(2,1)} %gather_fusion.4) | copy-start | bytes 1572868
  306.3 5.8 %copy-start.4 = (bf16[2048,128]{1,0:T(8,128)(2,1)S(1)}, bf16[2048,128]{1,0:T(8,128)(2,1)}, u32[]{:S(2)}) copy-start(bf16[2048,128]{1,0:T(8,128)(2,1)} %gather_fusion.5) | copy-start | bytes 1572868
  306.3 5.8 %copy-start.10 = (f32[256,2,4]{2,1,0:T(2,128)S(1)}, f32[256,2,4]{2,1,0:T(2,128)}, u32[]{:S(2)}) copy-start(f32[256,2,4]{2,1,0:T(2,128)} %copy.44) | copy-start | bytes 24580
  306.3 5.8 %copy-start.11 = (f32[256,2,4]{2,1,0:T(2,128)S(1)}, f32[256,2,4]{2,1,0:T(2,128)}, u32[]{:S(2)}) copy-start(f32[256,2,4]{2,1,0:T(2,128)} %copy.42) | copy-start | bytes 24580
  310.0 4.0 copy-start.12
  310.0 4.0 copy-start.13
  314.1 2.4 copy-start.16
  316.1 40.7 %copy-start.2 = (bf16[256,1024]{1,0:T(8,128)(2,1)S(1)}, bf16[256,1024]{1,0:T(8,128)(2,1)}, u32[]{:S(2)}) copy-start(bf16[256,1024]{1,0:T(8,128)(2,1)} %param.19) | copy-start | bytes 1572868
  317.9 47.4 %copy-start.20 = (f32[896]{0:T(1024)S(1)}, f32[896]{0:T(1024)}, u32[]{:S(2)}) copy-start(f32[896]{0:T(1024)} %param.29) | copy-start | bytes 10756
  317.9 69.8 %all-gather.2.cloned.1.call-start = ((), (), s32[]{:S(2)}) async-start(), calls=%async_computation.1 | async-start | bytes 2293760 | tf_op jit(solution)/shard_map/all_gather | solution.py:204
  390.6 8.1 %copy-start.24 = (f32[768]{0:T(1024)S(1)}, f32[768]{0:T(1024)}, u32[]{:S(2)}) copy-start(f32[768]{0:T(1024)} %param.31) | copy-start | bytes 9220
  449.4 6.3 %copy-start.14 = (f32[6,256,128]{2,1,0:T(8,128)S(1)}, f32[6,256,128]{2,1,0:T(8,128)}, u32[]{:S(2)}) copy-start(f32[6,256,128]{2,1,0:T(8,128)} %get-tuple-element.260) | copy-start | bytes 2359300 | tf_op jit(solution)/shard_map/while
  452.9 2.8 copy-start.1
  458.3 0.9 copy-start.15
  461.2 6.3 %copy-start.14 = (f32[6,256,128]{2,1,0:T(8,128)S(1)}, f32[6,256,128]{2,1,0:T(8,128)}, u32[]{:S(2)}) copy-start(f32[6,256,128]{2,1,0:T(8,128)} %get-tuple-element.260) | copy-start | bytes 2359300 | tf_op jit(solution)/shard_map/while
  464.7 2.8 copy-start.1
  470.1 0.9 copy-start.15
Sparse Core Ops, SparseCore 0:
  318.0 38.7 all-reduce.1
  366.4 21.2 all-gather.1
